TPU v7x, 32 devices: a whole 2x2x4 slice. The times are simulated.
32 devices in a mesh: groups: 2 (over y), row: 4 (over z), col: 4 (over x, core).
Axes of the slice: x: 2, y: 2, z: 4, core: 2. Of those that a mesh axis runs over, the one named last changes fastest.
Arguments:
- activations: bfloat16 [768, 4096], P(('groups', 'row'), 'col'), parts along dimension 0, may hold values from -52 to 52
- damping: float32 [8192], P(('groups', 'row')), parts along dimension 0, may hold values from 0.1 to 1
Outputs:
- factor: float32 [8192, 4096], P(('groups', 'row'), 'col'), parts along dimension 0
There are 2 independent parts, one for each index of `groups`. A program takes and returns all parts, laid end to end along the dimension named above; each array names one. Nothing has to cross between parts.
All inputs are finite; a program needn't handle non-finite values.
Results may differ from a plain program's by a relative error of at most 0.0003.
Values may be sent and summed in bfloat16 or wider, within the bound.
A program may use at most 64 MiB of HBM per device.

v0:
```python
import jax
import jax.numpy as jnp
from jax import lax
from jax.sharding import PartitionSpec as P

NB = 256
PANELS = 2
HIGHEST = lax.Precision.HIGHEST


def from_root(shard, axis, root):
    mine = lax.axis_index(axis) == root
    return lax.psum(jnp.where(mine, shard, jnp.zeros_like(shard)), axis)


def on_device(activations, damping):
    local_tokens = activations.shape[0]
    local_width = activations.shape[1]
    grid_size = lax.axis_size("row")
    row_dev = lax.axis_index("row")
    col_dev = lax.axis_index("col")
    columns = lax.all_gather(activations, "row", axis=0, tiled=True)
    mirrored = from_root(columns, "col", row_dev)
    gram_block = lax.dot_general(
        mirrored, columns, (((0,), (0,)), ((), ())), preferred_element_type=jnp.float32
    )
    diagonal_add = jnp.where(row_dev == col_dev, jnp.diag(damping), 0.0)
    matrix = gram_block / (local_tokens * grid_size) + diagonal_add
    local_index = jnp.arange(local_width, dtype=jnp.int32)
    global_rows = row_dev * local_width + local_index
    global_cols = col_dev * local_width + local_index

    def factor_step(panel_index, matrix):
        begin_at = panel_index * NB
        end_at = begin_at + NB
        owner_row = begin_at // local_width
        offset = begin_at - owner_row * local_width
        below = global_rows[:, None] >= end_at
        corner = lax.dynamic_slice(matrix, (offset, offset), (NB, NB))
        corner = lax.psum(jnp.where(row_dev == owner_row, corner, 0.0), "row")
        safe_corner = jnp.where(col_dev == owner_row, corner, jnp.eye(NB, dtype=jnp.float32))
        pivot_block = jnp.linalg.cholesky(safe_corner)
        own_block = lax.dynamic_slice_in_dim(matrix, offset, NB, 1)
        solved = jax.scipy.linalg.solve_triangular(pivot_block, own_block.T, lower=True).T
        row_side = lax.psum(jnp.where(col_dev == owner_row, solved, 0.0), "col")
        trail_rows = jnp.where(below, row_side, 0.0)
        trail_cols = lax.psum(jnp.where(row_dev == col_dev, trail_rows, 0.0), "row")
        trail_colsT = trail_cols.T
        update = jnp.dot(
            trail_rows, trail_colsT, precision=HIGHEST, preferred_element_type=jnp.float32
        )
        matrix = matrix - update
        placed = lax.dynamic_update_slice(trail_rows, pivot_block, (offset, 0))
        panel_rows = jnp.where(row_dev == owner_row, placed, trail_rows)
        written = lax.dynamic_update_slice(matrix, panel_rows, (0, offset))
        matrix = jnp.where(col_dev == owner_row, written, matrix)
        in_block = (global_rows[:, None] >= begin_at) & (global_rows[:, None] < end_at)
        right_side = global_cols[None, :] >= end_at
        return jnp.where(in_block & right_side, 0.0, matrix)

    return lax.fori_loop(0, PANELS, factor_step, matrix)


def solution(mesh):
    in_specs = (P(("groups", "row"), "col"), P(("groups", "row")))
    out_specs = P(("groups", "row"), "col")
    return jax.shard_map(
        on_device, mesh=mesh, in_specs=in_specs, out_specs=out_specs, check_vma=False
    )
```

profile of v0, /device:TPU:0, one launch (start us, length us, event | category | flops | bytes accessed | tf_op | source)
XLA Modules:
  0.0 492.9 jit_solution(14677081952462626796)
XLA Ops:
  6.5 21.5 %all_gather.3 = bf16[384,1024]{1,0:T(8,128)(2,1)S(1)} all-gather(bf16[96,1024]{1,0:T(8,128)(2,1)} %param.4), channel_id=1, replica_groups=mesh['groups'=2,'row'=4,'col'=4] {'row'}, dimensions={0}, use_global_device_ids=true | all-gather | bytes 983040 | tf_op jit(solution)/shard_map/all_gather | solution.py:22
  29.0 34.5 %all-reduce.6.cloned.1.call-done = bf16[384,1024]{1,0:T(8,128)(2,1)} async-done(((bf16[384,1024]{1,0:T(8,128)(2,1)}), bf16[384,1024]{1,0:T(8,128)(2,1)}) %all-reduce.6.cloned.1.call-update) | async-done | bytes 786448 | tf_op jit(solution)/shard_map/psum | solution.py:13
  63.5 4.4 select_add_fusion
  68.0 5.3 %copy.9 = f32[1024,1024]{0,1:T(8,128)} copy(f32[1024,1024]{1,0:T(8,128)} %select_add_fusion) | data formatting | bytes 8388608
  73.3 407.4 %while.20 = (s32[]{:T(128)}, f32[1024,1024]{0,1:T(8,128)}, s32[]{:T(128)}, s32[]{:T(128)}, pred[]{:T(512)}, /*index=5*/s32[]{:T(128)}, s32[]{:T(128)}, s32[]{:T(...) while((s32[]{:T(128)}, f32[1024,1024]{0,1:T(8,128)}, ...), condition=%wide.region_9.10_spmd.clone, body=%wide.region_1.9_spmd.clone.sunk | while | flops 3881984256 | bytes 53224180 | solution.py:61
  73.3 1.7 dynamic-slice_select_fusion.2
  76.4 35.7 %all-reduce.8.cloned.1.call-done = f32[256,256]{0,1:T(8,128)} async-done(((f32[256,256]{0,1:T(8,128)}), f32[256,256]{0,1:T(8,128)}) %all-reduce.8.cloned.1.call-update) | async-done | bytes 262160 | tf_op jit(solution)/shard_map/while/body/eval_jaxpr/psum | solution.py:40
  114.2 11.7 %cholesky.225 = f32[128,128]{1,0:T(8,128)S(1)} custom-call(f32[128,128]{1,0:T(8,128)S(1)} %cholesky.224), custom_call_target="Cholesky" | custom-call | tf_op jit(solution)/shard_map/while/body/eval_jaxpr/jit(cholesky)/cholesky | solution.py:42
  126.0 9.8 %custom-call.49 = f32[1,128,128]{1,2,0:T(8,128)S(1)} custom-call(f32[1,128,128]{2,1,0:T(8,128)S(1)} %get-tuple-element.322), custom_call_target="InvertDiagBlocksLowerTriangular" | custom-call | tf_op jit(solution)/shard_map/while/body/eval_jaxpr/jit(cholesky)/cholesky | solution.py:42
  136.3 11.7 %cholesky.227 = f32[128,128]{1,0:T(8,128)S(1)} custom-call(f32[128,128]{1,0:T(8,128)S(1)} %convolution_subtract_fusion.6), custom_call_target="Cholesky" | custom-call | tf_op jit(solution)/shard_map/while/body/eval_jaxpr/jit(cholesky)/cholesky | solution.py:42
  150.4 4.2 while.21
  151.0 1.4 dynamic-slice.21
  154.6 19.7 %custom-call.51 = f32[2,128,128]{1,2,0:T(8,128)S(1)} custom-call(f32[2,128,128]{2,1,0:T(8,128)S(1)} %get-tuple-element.326), custom_call_target="InvertDiagBlocksLowerTriangular" | custom-call | tf_op jit(solution)/shard_map/while/body/eval_jaxpr/jit(_solve_triangular)/triangular_solve | solution.py:44
  177.3 35.3 %all-reduce.10.cloned.1.call-done = f32[1024,256]{0,1:T(8,128)} async-done(((f32[1024,256]{0,1:T(8,128)}), f32[1024,256]{0,1:T(8,128)}) %all-reduce.10.cloned.1.call-update) | async-done | bytes 1048592 | tf_op jit(solution)/shard_map/while/body/eval_jaxpr/psum | solution.py:45
  212.7 2.5 broadcast_select_fusion.5
  215.2 52.5 %all-reduce.12.cloned.1.call-done = f32[1024,256]{0,1:T(8,128)} async-done(((f32[1024,256]{0,1:T(8,128)}), f32[1024,256]{0,1:T(8,128)}) %all-reduce.12.cloned.1.call-update) | async-done | bytes 1048592 | tf_op jit(solution)/shard_map/while/body/eval_jaxpr/psum | solution.py:47
  267.7 7.2 %convolution_subtract_fusion.8 = f32[1024,1024]{0,1:T(8,128)S(1)} fusion(f32[1024,1024]{0,1:T(8,128)} %get-tuple-element.370, f32[1024,256]{0,1:T(8,128)S(1)} %get-tuple-element.327, f32[1024,256]{0,1:T(8,128)} %all-reduce.12.cloned.1.call-done), kind=kOutput, calls=%fused_computation.5.clone.1 | convolution fusion | flops 3222274048 | bytes 10485760 | tf_op jit(solution)/shard_map/while/body/eval_jaxpr/dot_general | solution.py:49
  275.1 2.4 and_select_fusion.2
  277.5 1.7 dynamic-slice_select_fusion.2
  280.6 34.6 %all-reduce.8.cloned.1.call-done = f32[256,256]{0,1:T(8,128)} async-done(((f32[256,256]{0,1:T(8,128)}), f32[256,256]{0,1:T(8,128)}) %all-reduce.8.cloned.1.call-update) | async-done | bytes 262160 | tf_op jit(solution)/shard_map/while/body/eval_jaxpr/psum | solution.py:40
  317.4 11.7 %cholesky.225 = f32[128,128]{1,0:T(8,128)S(1)} custom-call(f32[128,128]{1,0:T(8,128)S(1)} %cholesky.224), custom_call_target="Cholesky" | custom-call | tf_op jit(solution)/shard_map/while/body/eval_jaxpr/jit(cholesky)/cholesky | solution.py:42
  329.1 9.8 %custom-call.49 = f32[1,128,128]{1,2,0:T(8,128)S(1)} custom-call(f32[1,128,128]{2,1,0:T(8,128)S(1)} %get-tuple-element.322), custom_call_target="InvertDiagBlocksLowerTriangular" | custom-call | tf_op jit(solution)/shard_map/while/body/eval_jaxpr/jit(cholesky)/cholesky | solution.py:42
  339.4 11.7 %cholesky.227 = f32[128,128]{1,0:T(8,128)S(1)} custom-call(f32[128,128]{1,0:T(8,128)S(1)} %convolution_subtract_fusion.6), custom_call_target="Cholesky" | custom-call | tf_op jit(solution)/shard_map/while/body/eval_jaxpr/jit(cholesky)/cholesky | solution.py:42
  353.6 4.2 while.21
  354.2 1.4 dynamic-slice.21
  357.7 19.7 %custom-call.51 = f32[2,128,128]{1,2,0:T(8,128)S(1)} custom-call(f32[2,128,128]{2,1,0:T(8,128)S(1)} %get-tuple-element.326), custom_call_target="InvertDiagBlocksLowerTriangular" | custom-call | tf_op jit(solution)/shard_map/while/body/eval_jaxpr/jit(_solve_triangular)/triangular_solve | solution.py:44
  380.5 35.3 %all-reduce.10.cloned.1.call-done = f32[1024,256]{0,1:T(8,128)} async-done(((f32[1024,256]{0,1:T(8,128)}), f32[1024,256]{0,1:T(8,128)}) %all-reduce.10.cloned.1.call-update) | async-done | bytes 1048592 | tf_op jit(solution)/shard_map/while/body/eval_jaxpr/psum | solution.py:45
  415.8 2.5 broadcast_select_fusion.5
  418.3 52.5 %all-reduce.12.cloned.1.call-done = f32[1024,256]{0,1:T(8,128)} async-done(((f32[1024,256]{0,1:T(8,128)}), f32[1024,256]{0,1:T(8,128)}) %all-reduce.12.cloned.1.call-update) | async-done | bytes 1048592 | tf_op jit(solution)/shard_map/while/body/eval_jaxpr/psum | solution.py:47
  470.8 7.2 %convolution_subtract_fusion.8 = f32[1024,1024]{0,1:T(8,128)S(1)} fusion(f32[1024,1024]{0,1:T(8,128)} %get-tuple-element.370, f32[1024,256]{0,1:T(8,128)S(1)} %get-tuple-element.327, f32[1024,256]{0,1:T(8,128)} %all-reduce.12.cloned.1.call-done), kind=kOutput, calls=%fused_computation.5.clone.1 | convolution fusion | flops 3222274048 | bytes 10485760 | tf_op jit(solution)/shard_map/while/body/eval_jaxpr/dot_general | solution.py:49
  478.3 2.4 and_select_fusion.2
  480.7 5.3 %copy.10 = f32[1024,1024]{1,0:T(8,128)} copy(f32[1024,1024]{0,1:T(8,128)} %get-tuple-element.167) | data formatting | bytes 8388608 | tf_op jit(solution)/shard_map/while | solution.py:61
  (89 shorter events, 23.2 us)
Async XLA Ops:
  6.5 57.0 %all-reduce.6.cloned.1.call-start = ((), (), s32[]{:S(2)}) async-start(), calls=%async_computation | async-start | bytes 1572864 | tf_op jit(solution)/shard_map/psum | solution.py:13
  73.3 38.8 %all-reduce.8.cloned.1.call-start = ((), (), s32[]{:S(2)}) async-start(), calls=%async_computation.1 | async-start | bytes 524288 | tf_op jit(solution)/shard_map/while/body/eval_jaxpr/psum | solution.py:40
  75.0 137.7 %all-reduce.10.cloned.1.call-start = ((), (), s32[]{:S(2)}) async-start(), calls=%async_computation.2 | async-start | bytes 2097152 | tf_op jit(solution)/shard_map/while/body/eval_jaxpr/psum | solution.py:45
  177.2 90.4 %all-reduce.12.cloned.1.call-start = ((), (), s32[]{:S(2)}) async-start(), calls=%async_computation.3 | async-start | bytes 2097152 | tf_op jit(solution)/shard_map/while/body/eval_jaxpr/psum | solution.py:47
  277.5 37.7 %all-reduce.8.cloned.1.call-start = ((), (), s32[]{:S(2)}) async-start(), calls=%async_computation.1 | async-start | bytes 524288 | tf_op jit(solution)/shard_map/while/body/eval_jaxpr/psum | solution.py:40
  279.2 136.6 %all-reduce.10.cloned.1.call-start = ((), (), s32[]{:S(2)}) async-start(), calls=%async_computation.2 | async-start | bytes 2097152 | tf_op jit(solution)/shard_map/while/body/eval_jaxpr/psum | solution.py:45
  380.4 90.4 %all-reduce.12.cloned.1.call-start = ((), (), s32[]{:S(2)}) async-start(), calls=%async_computation.3 | async-start | bytes 2097152 | tf_op jit(solution)/shard_map/while/body/eval_jaxpr/psum | solution.py:47
Sparse Core Ops, SparseCore 0:
  29.1 34.3 all-reduce.5
  76.4 35.5 all-reduce.7
  177.4 35.2 all-reduce.9
  215.3 52.3 all-reduce.11
  280.3 34.8 all-reduce.7
  380.5 35.2 all-reduce.9
  418.4 52.3 all-reduce.11
where the time goes:
time: 494 us; the launch traced here: 493 us
  waiting for transfers between devices  281 us (57%)
  other arithmetic  128 us (26%)
  matrix products  23.5 us (5%)
  local copies, waits for them, and re-layouts  22.5 us (5%)
  blocking collectives  21.5 us (4%)
  between operations  13.4 us (3%)
    psum x2, waiting for transfers between devices, factor_step(): trail_cols = lax.psum(jnp.where(row_dev == col_dev, trail_rows, 0.0), 'row')  105 us
    psum x2, waiting for transfers between devices, factor_step(): row_side = lax.psum(jnp.where(col_dev == owner_row, solved, 0.0), 'col')  70.7 us
    psum x2, waiting for transfers between devices, factor_step(): corner = lax.psum(jnp.where(row_dev == owner_row, corner, 0.0), 'row')  70.3 us
    another operation x12, other arithmetic, factor_step(): pivot_block = jnp.linalg.cholesky(safe_corner)  67.9 us
    another operation x6, other arithmetic, factor_step(): jax.scipy.linalg.solve_triangular(pivot_block, own_block.T, lower=True)  39.4 us
    psum x1, waiting for transfers between devices, from_root(): return lax.psum(jnp.where(mine, shard, jnp.zeros_like(shard)), axis)  34.5 us
    all_gather x1, blocking collectives, on_device(): columns = lax.all_gather(activations, 'row', axis=0, tiled=True)  21.5 us
    dot_general x2, matrix products, factor_step(): jnp.dot(trail_rows, trail_colsT, precision=HIGHEST, preferred_element_typ...  14.3 us
  transfers between devices with their start and end apart: 7, of which 7 were waited for; matrix products, arithmetic and copies ran while one was open for 1% of the time, Pallas kernels for 0%

commit v1 on v0

--- a/solution.py
+++ b/solution.py
@@ -6,6 +6,12 @@
 NB = 256
 PANELS = 2
 HIGHEST = lax.Precision.HIGHEST
+
+
+def gather_and_add(x, mesh_axis):
+    parts = lax.all_gather(x, mesh_axis, axis=0, tiled=False)
+    summed = parts.sum(axis=0)
+    return summed
 
 
 def from_root(shard, axis, root):
@@ -44,7 +50,7 @@
         solved = jax.scipy.linalg.solve_triangular(pivot_block, own_block.T, lower=True).T
         row_side = lax.psum(jnp.where(col_dev == owner_row, solved, 0.0), "col")
         trail_rows = jnp.where(below, row_side, 0.0)
-        trail_cols = lax.psum(jnp.where(row_dev == col_dev, trail_rows, 0.0), "row")
+        trail_cols = gather_and_add(jnp.where(row_dev == col_dev, trail_rows, 0.0), "row")
         trail_colsT = trail_cols.T
         update = jnp.dot(
             trail_rows, trail_colsT, precision=HIGHEST, preferred_element_type=jnp.float32

time: 494 us -> 569 us (1.15)
  waiting for transfers between devices: 281 us -> 338 us
  local copies, waits for them, and re-layouts: 22.5 us -> 34.5 us
  other arithmetic: 128 us -> 137 us
    all_gather x0 -> x2, waiting for transfers between devices: none -> 163 us  [gather_and_add(): parts = lax.all_gather(x, mesh_axis, axis=0, tiled=False)]
    psum x2 -> x0, waiting for transfers between devices: 105 us -> none  [factor_step(): trail_cols = lax.psum(jnp.where(row_dev == col_dev, trail_rows, 0.0), 'row')]
    all_gather x0 -> x2, local copies, waits for them, and re-layouts: none -> 12 us  [gather_and_add(): parts = lax.all_gather(x, mesh_axis, axis=0, tiled=False)]
    reduce_sum x0 -> x2, other arithmetic: none -> 9.48 us  [gather_and_add(): summed = parts.sum(axis=0)]
  transfers between devices with their start and end apart: 7 -> 7, of which waited for: 7 -> 7; matrix products, arithmetic and copies ran while one was open for 1% -> 0% of each run, Pallas kernels for 0% -> 0%
where the time goes in v1:
time: 569 us; the launch traced here: 568 us
  waiting for transfers between devices  338 us (59%)
  other arithmetic  137 us (24%)
  local copies, waits for them, and re-layouts  34.5 us (6%)
  blocking collectives  21.5 us (4%)
  matrix products  20 us (4%)
  between operations  13.4 us (2%)
    all_gather x2, waiting for transfers between devices, gather_and_add(): parts = lax.all_gather(x, mesh_axis, axis=0, tiled=False)  163 us
    psum x2, waiting for transfers between devices, factor_step(): row_side = lax.psum(jnp.where(col_dev == owner_row, solved, 0.0), 'col')  70.7 us
    psum x2, waiting for transfers between devices, factor_step(): corner = lax.psum(jnp.where(row_dev == owner_row, corner, 0.0), 'row')  69.5 us
    another operation x12, other arithmetic, factor_step(): pivot_block = jnp.linalg.cholesky(safe_corner)  67.9 us
    another operation x6, other arithmetic, factor_step(): jax.scipy.linalg.solve_triangular(pivot_block, own_block.T, lower=True)  39.4 us
    psum x1, waiting for transfers between devices, from_root(): return lax.psum(jnp.where(mine, shard, jnp.zeros_like(shard)), axis)  34.5 us
    all_gather x1, blocking collectives, on_device(): columns = lax.all_gather(activations, 'row', axis=0, tiled=True)  21.5 us
    all_gather x2, local copies, waits for them, and re-layouts, gather_and_add(): parts = lax.all_gather(x, mesh_axis, axis=0, tiled=False)  12 us
  transfers between devices with their start and end apart: 7, of which 7 were waited for; matrix products, arithmetic and copies ran while one was open for 0% of the time, Pallas kernels for 0%

profile of v1, /device:TPU:0, one launch (start us, length us, event | category | flops | bytes accessed | tf_op | source)
XLA Modules:
  0.0 567.7 jit_solution(234010666290158842)
XLA Ops:
  6.5 21.5 %all_gather.23 = bf16[384,1024]{1,0:T(8,128)(2,1)S(1)} all-gather(bf16[96,1024]{1,0:T(8,128)(2,1)} %param.4), channel_id=1, replica_groups=mesh['groups'=2,'row'=4,'col'=4] {'row'}, dimensions={0}, use_global_device_ids=true | all-gather | bytes 983040 | tf_op jit(solution)/shard_map/all_gather | solution.py:28
  29.0 34.5 %all-reduce.5.cloned.1.call-done = bf16[384,1024]{1,0:T(8,128)(2,1)} async-done(((bf16[384,1024]{1,0:T(8,128)(2,1)}), bf16[384,1024]{1,0:T(8,128)(2,1)}) %all-reduce.5.cloned.1.call-update) | async-done | bytes 786448 | tf_op jit(solution)/shard_map/psum | solution.py:19
  63.5 4.4 select_add_fusion
  68.0 5.3 copy.17
  73.3 482.2 %while.20 = (s32[]{:T(128)}, f32[1024,1024]{0,1:T(8,128)}, s32[]{:T(128)}, s32[]{:T(128)}, pred[]{:T(512)}, /*index=5*/s32[]{:T(128)}, s32[]{:T(128)}, s32[]{:T(...) while((s32[]{:T(128)}, f32[1024,1024]{0,1:T(8,128)}, ...), condition=%wide.region_9.10_spmd.clone, body=%wide.region_1.9_spmd.clone.sunk | while | flops 3882508544 | bytes 76292872 | solution.py:67
  76.4 35.7 %all-reduce.7.cloned.1.call-done = f32[256,256]{0,1:T(8,128)} async-done(((f32[256,256]{0,1:T(8,128)}), f32[256,256]{0,1:T(8,128)}) %all-reduce.7.cloned.1.call-update) | async-done | bytes 262160 | tf_op jit(solution)/shard_map/while/body/eval_jaxpr/psum | solution.py:46
  114.2 11.7 %cholesky.225 = f32[128,128]{1,0:T(8,128)S(1)} custom-call(f32[128,128]{1,0:T(8,128)S(1)} %cholesky.224), custom_call_target="Cholesky" | custom-call | tf_op jit(solution)/shard_map/while/body/eval_jaxpr/jit(cholesky)/cholesky | solution.py:48
  126.1 9.8 %custom-call.49 = f32[1,128,128]{1,2,0:T(8,128)S(1)} custom-call(f32[1,128,128]{2,1,0:T(8,128)S(1)} %get-tuple-element.333), custom_call_target="InvertDiagBlocksLowerTriangular" | custom-call | tf_op jit(solution)/shard_map/while/body/eval_jaxpr/jit(cholesky)/cholesky | solution.py:48
  136.5 11.7 %cholesky.227 = f32[128,128]{1,0:T(8,128)S(1)} custom-call(f32[128,128]{1,0:T(8,128)S(1)} %convolution_subtract_fusion.6), custom_call_target="Cholesky" | custom-call | tf_op jit(solution)/shard_map/while/body/eval_jaxpr/jit(cholesky)/cholesky | solution.py:48
  150.4 4.2 while.21
  154.6 19.7 %custom-call.51 = f32[2,128,128]{1,2,0:T(8,128)S(1)} custom-call(f32[2,128,128]{2,1,0:T(8,128)S(1)} %get-tuple-element.337), custom_call_target="InvertDiagBlocksLowerTriangular" | custom-call | tf_op jit(solution)/shard_map/while/body/eval_jaxpr/jit(_solve_triangular)/triangular_solve | solution.py:50
  177.3 35.3 %all-reduce.9.cloned.1.call-done = f32[1024,256]{0,1:T(8,128)} async-done(((f32[1024,256]{0,1:T(8,128)}), f32[1024,256]{0,1:T(8,128)}) %all-reduce.9.cloned.1.call-update) | async-done | bytes 1048592 | tf_op jit(solution)/shard_map/while/body/eval_jaxpr/psum | solution.py:51
  212.7 2.5 broadcast_select_fusion.5
  215.2 81.3 %all-gather.6.cloned.1.call-done = f32[4096,256]{0,1:T(8,128)} async-done(((f32[1024,256]{0,1:T(8,128)}), f32[4096,256]{0,1:T(8,128)}) %all-gather.6.cloned.1.call-update) | async-done | bytes 4194320 | tf_op jit(solution)/shard_map/while/body/eval_jaxpr/all_gather | solution.py:12
  296.5 6.0 %reshape.113 = f32[4,1024,256]{1,0,2:T(4,128)} reshape(f32[4096,256]{0,1:T(8,128)} %all-gather.6.cloned.1.call-done) | data formatting | bytes 8388608 | tf_op jit(solution)/shard_map/while/body/eval_jaxpr/all_gather | solution.py:12
  302.5 4.7 reduce_sum.18
  307.3 5.4 convolution_subtract_fusion.8
  313.0 2.4 and_select_fusion.2
  318.4 33.8 %all-reduce.7.cloned.1.call-done = f32[256,256]{0,1:T(8,128)} async-done(((f32[256,256]{0,1:T(8,128)}), f32[256,256]{0,1:T(8,128)}) %all-reduce.7.cloned.1.call-update) | async-done | bytes 262160 | tf_op jit(solution)/shard_map/while/body/eval_jaxpr/psum | solution.py:46
  354.4 11.7 %cholesky.225 = f32[128,128]{1,0:T(8,128)S(1)} custom-call(f32[128,128]{1,0:T(8,128)S(1)} %cholesky.224), custom_call_target="Cholesky" | custom-call | tf_op jit(solution)/shard_map/while/body/eval_jaxpr/jit(cholesky)/cholesky | solution.py:48
  366.3 9.8 %custom-call.49 = f32[1,128,128]{1,2,0:T(8,128)S(1)} custom-call(f32[1,128,128]{2,1,0:T(8,128)S(1)} %get-tuple-element.333), custom_call_target="InvertDiagBlocksLowerTriangular" | custom-call | tf_op jit(solution)/shard_map/while/body/eval_jaxpr/jit(cholesky)/cholesky | solution.py:48
  376.7 11.7 %cholesky.227 = f32[128,128]{1,0:T(8,128)S(1)} custom-call(f32[128,128]{1,0:T(8,128)S(1)} %convolution_subtract_fusion.6), custom_call_target="Cholesky" | custom-call | tf_op jit(solution)/shard_map/while/body/eval_jaxpr/jit(cholesky)/cholesky | solution.py:48
  390.6 4.2 while.21
  394.8 19.7 %custom-call.51 = f32[2,128,128]{1,2,0:T(8,128)S(1)} custom-call(f32[2,128,128]{2,1,0:T(8,128)S(1)} %get-tuple-element.337), custom_call_target="InvertDiagBlocksLowerTriangular" | custom-call | tf_op jit(solution)/shard_map/while/body/eval_jaxpr/jit(_solve_triangular)/triangular_solve | solution.py:50
  417.5 35.3 %all-reduce.9.cloned.1.call-done = f32[1024,256]{0,1:T(8,128)} async-done(((f32[1024,256]{0,1:T(8,128)}), f32[1024,256]{0,1:T(8,128)}) %all-reduce.9.cloned.1.call-update) | async-done | bytes 1048592 | tf_op jit(solution)/shard_map/while/body/eval_jaxpr/psum | solution.py:51
  452.8 2.5 broadcast_select_fusion.5
  455.3 81.3 %all-gather.6.cloned.1.call-done = f32[4096,256]{0,1:T(8,128)} async-done(((f32[1024,256]{0,1:T(8,128)}), f32[4096,256]{0,1:T(8,128)}) %all-gather.6.cloned.1.call-update) | async-done | bytes 4194320 | tf_op jit(solution)/shard_map/while/body/eval_jaxpr/all_gather | solution.py:12
  536.7 6.0 %reshape.113 = f32[4,1024,256]{1,0,2:T(4,128)} reshape(f32[4096,256]{0,1:T(8,128)} %all-gather.6.cloned.1.call-done) | data formatting | bytes 8388608 | tf_op jit(solution)/shard_map/while/body/eval_jaxpr/all_gather | solution.py:12
  542.7 4.7 reduce_sum.18
  547.5 5.4 convolution_subtract_fusion.8
  553.1 2.4 and_select_fusion.2
  555.6 5.3 copy.18
  (93 shorter events, 29.3 us)
Async XLA Ops:
  6.5 57.0 %all-reduce.5.cloned.1.call-start = ((), (), s32[]{:S(2)}) async-start(), calls=%async_computation | async-start | bytes 1572864 | tf_op jit(solution)/shard_map/psum | solution.py:19
  73.3 38.8 %all-reduce.7.cloned.1.call-start = ((), (), s32[]{:S(2)}) async-start(), calls=%async_computation.1 | async-start | bytes 524288 | tf_op jit(solution)/shard_map/while/body/eval_jaxpr/psum | solution.py:46
  75.0 137.6 %all-reduce.9.cloned.1.call-start = ((), (), s32[]{:S(2)}) async-start(), calls=%async_computation.2 | async-start | bytes 2097152 | tf_op jit(solution)/shard_map/while/body/eval_jaxpr/psum | solution.py:51
  177.2 119.3 %all-gather.6.cloned.1.call-start = ((), (), s32[]{:S(2)}) async-start(), calls=%async_computation.3 | async-start | bytes 5242880 | tf_op jit(solution)/shard_map/while/body/eval_jaxpr/all_gather | solution.py:12
  315.4 36.9 %all-reduce.7.cloned.1.call-start = ((), (), s32[]{:S(2)}) async-start(), calls=%async_computation.1 | async-start | bytes 524288 | tf_op jit(solution)/shard_map/while/body/eval_jaxpr/psum | solution.py:46
  317.1 135.8 %all-reduce.9.cloned.1.call-start = ((), (), s32[]{:S(2)}) async-start(), calls=%async_computation.2 | async-start | bytes 2097152 | tf_op jit(solution)/shard_map/while/body/eval_jaxpr/psum | solution.py:51
  417.4 119.3 %all-gather.6.cloned.1.call-start = ((), (), s32[]{:S(2)}) async-start(), calls=%async_computation.3 | async-start | bytes 5242880 | tf_op jit(solution)/shard_map/while/body/eval_jaxpr/all_gather | solution.py:12
Sparse Core Ops, SparseCore 0:
  29.1 34.3 all-reduce.4
  76.4 35.5 all-reduce.6
  177.4 35.2 all-reduce.8
  215.3 81.2 all-gather.5
  318.2 34.0 all-reduce.6
  417.6 35.2 all-reduce.8
  455.5 81.2 all-gather.5
